TPU v7x, 32 devices: a whole 2x2x4 slice. The times are simulated.
32 devices in a mesh: pair: 2 (over y), rep: 4 (over x, core), blk: 4 (over z).
Axes of the slice: x: 2, y: 2, z: 4, core: 2. Of those that a mesh axis runs over, the one named last changes fastest.
Arguments:
- src_spectra: bfloat16 [64, 8192], P(None, ('pair', 'rep', 'blk')), parts along dimension 1, may hold values from -4 to 4
- tgt_spectra: bfloat16 [64, 8192], P(None, ('pair', 'blk')), parts along dimension 1, may hold values from -4 to 4
- log_src_weight: float32 [8192], P(('pair', 'rep', 'blk')), parts along dimension 0, may hold values from -2 to 2
- log_tgt_weight: float32 [8192], P(('pair', 'blk')), parts along dimension 0, may hold values from -2 to 2
- src_potential: float32 [8192], P(('pair', 'rep', 'blk')), parts along dimension 0, may hold values from -4 to 250
- tgt_potential: float32 [8192], P(('pair', 'blk')), parts along dimension 0, may hold values from -4 to 250
Outputs:
- src_updated: float32 [8192], P(('pair', 'rep', 'blk')), parts along dimension 0
- tgt_updated: float32 [8192], P(('pair', 'blk')), parts along dimension 0
There are 2 independent parts, one for each index of `pair`. A program takes and returns all parts, laid end to end along the dimension named above; each array names one. Nothing has to cross between parts.
All inputs are finite; a program needn't handle non-finite values.
Results may differ from a plain program's by a relative error of at most 0.0003.
Values may be sent and summed in bfloat16 or wider, within the bound.
No kernel may reach another device: no remote copies, remote signals or barrier semaphores. Data moves between devices by JAX's collectives and lax.ppermute only.
A program may use at most 128 MiB of HBM per device.

v0:
```python
import jax
import jax.numpy as jnp
from jax import lax
from jax.sharding import PartitionSpec as P


def passed_along(value, axis, steps):
    count = lax.axis_size(axis)
    pairs = [(source, (source + steps) % count) for source in range(count)]
    return lax.ppermute(value, axis, pairs)


def merged(value, axis, join):
    pieces = jax.tree.map(lambda part: lax.all_gather(part, axis), value)
    head = jax.tree.map(lambda part: part[0], pieces)
    tail = jax.tree.map(lambda part: part[1:], pieces)
    so_far, _ = lax.scan(lambda so_far, share: (join(so_far, share), None), head, tail)
    return so_far


def peaks_join(earlier, later):
    joined = jnp.maximum(earlier[0], later[0])
    return (
        joined,
        earlier[1] * jnp.exp(earlier[0] - joined) + later[1] * jnp.exp(later[0] - joined),
    )


def tile_scores(src_spectra, src_square, src_bias, tgt_bias, spectra_piece, offset):
    width = spectra_piece.shape[1]
    piece_float = spectra_piece.astype(jnp.float32)
    tgt_square = 0.5 * jnp.sum(piece_float * piece_float, axis=0)
    products = lax.dot_general(
        src_spectra, spectra_piece, (((0,), (0,)), ((), ())), preferred_element_type=jnp.float32
    )
    cost_tile = src_square[:, None] + tgt_square[None, :] - products
    bias_piece = lax.dynamic_slice_in_dim(tgt_bias, offset, width, 0)
    return (bias_piece[None, :] - cost_tile, src_bias[:, None] - cost_tile)


def row_update(row_peak, row_totals, row_scores):
    joined = jnp.maximum(row_peak, jnp.max(row_scores, axis=1))
    fresh = jnp.sum(jnp.exp(row_scores - joined[:, None]), axis=1)
    return (joined, row_totals * jnp.exp(row_peak - joined) + fresh)


def column_part(col_scores):
    block_peak = jnp.max(col_scores, axis=0)
    return (block_peak, jnp.sum(jnp.exp(col_scores - block_peak[None, :]), axis=0))


def on_device(
    src_spectra, tgt_spectra, log_src_weight, log_tgt_weight, src_potential, tgt_potential
):
    src_float = src_spectra.astype(jnp.float32)
    src_square = 0.5 * jnp.sum(src_float * src_float, axis=0)
    src_bias = log_src_weight + src_potential
    tgt_bias = lax.all_gather(log_tgt_weight + tgt_potential, "blk", axis=0, tiled=True)
    own_width = tgt_spectra.shape[1]
    everything = tgt_bias.shape[0]
    rows_here = src_spectra.shape[1]
    start_peak = jnp.full((rows_here,), -jnp.inf, jnp.float32)
    start_totals = jnp.zeros((rows_here,), jnp.float32)
    shards = everything // own_width
    home = lax.axis_index("blk")

    def turn(turn_index, carry):
        row_peak, row_totals, spectra_piece, carried_peak, carried_totals = carry
        offset = (home - turn_index) % shards * own_width
        row_scores, col_scores = tile_scores(
            src_spectra, src_square, src_bias, tgt_bias, spectra_piece, offset
        )
        row_peak, row_totals = row_update(row_peak, row_totals, row_scores)
        carried_peak, carried_totals = peaks_join(
            (carried_peak, carried_totals), column_part(col_scores)
        )
        spectra_piece = passed_along(spectra_piece, "blk", 1)
        carried_peak, carried_totals = passed_along((carried_peak, carried_totals), "blk", 1)
        return (row_peak, row_totals, spectra_piece, carried_peak, carried_totals)

    carry = (
        start_peak,
        start_totals,
        tgt_spectra,
        jnp.full((own_width,), -jnp.inf, jnp.float32),
        jnp.zeros((own_width,), jnp.float32),
    )
    row_peak, row_totals, returned, carried_peak, carried_totals = lax.fori_loop(
        0, shards, turn, carry
    )
    mine_peak, mine_totals = merged((carried_peak, carried_totals), "rep", peaks_join)
    tgt_new = -(mine_peak + jnp.log(mine_totals))
    src_new = -(row_peak + jnp.log(row_totals))
    return (0.5 * (src_potential + src_new), 0.5 * (tgt_potential + tgt_new))


def solution(mesh):
    placed = (
        P(None, ("pair", "rep", "blk")),
        P(None, ("pair", "blk")),
        P(("pair", "rep", "blk")),
        P(("pair", "blk")),
        P(("pair", "rep", "blk")),
        P(("pair", "blk")),
    )
    return jax.shard_map(
        on_device,
        mesh=mesh,
        in_specs=placed,
        out_specs=(P(("pair", "rep", "blk")), P(("pair", "blk"))),
        check_vma=False,
    )
```

profile of v0, /device:TPU:0, one launch (start us, length us, event | category | flops | bytes accessed | tf_op | source)
XLA Modules:
  0.0 62.2 jit_solution(9020351512151376552)
XLA Ops:
  0.7 0.7 %copy-done.3 = f32[1024]{0:T(1024)S(1)} copy-done((f32[1024]{0:T(1024)S(1)}, f32[1024]{0:T(1024)}, u32[]{:S(2)}) %copy-start.3) | copy-done | bytes 4120
  1.4 14.9 %all_gather.15 = f32[4096]{0:T(1024)S(1)} all-gather(f32[1024]{0:T(1024)S(1)} %add.130), channel_id=1, replica_groups=mesh['pair'=2,'rep'=4,'blk'=4] {'blk'}, dimensions={0}, use_global_device_ids=true | all-gather | bytes 20480 | tf_op jit(solution)/shard_map/all_gather | solution.py:58
  16.4 0.7 %copy-done.6 = f32[256]{0:T(256)S(1)} copy-done((f32[256]{0:T(256)S(1)}, f32[256]{0:T(256)}, u32[]{:S(2)}) %copy-start.6) | copy-done | bytes 1048
  17.0 32.7 %while.37 = (s32[]{:T(128)}, f32[256]{0:T(256)S(1)}, f32[256]{0:T(256)S(1)}, bf16[64,1024]{1,0:T(8,128)(2,1)S(1)}, f32[1024]{0:T(1024)S(1)}, /*index=5*/f32[1024...) while((s32[]{:T(128)}, f32[256]{0:T(256)S(1)}, ...), condition=%wide.region_7.8_spmd.clone, body=%wide.region_1.7_spmd.clone.sunk | while | flops 36902160 | bytes 3297739 | solution.py:88
  17.1 1.6 %collective-permute-start = (bf16[64,1024]{1,0:T(8,128)(2,1)S(1)}, bf16[64,1024]{1,0:T(8,128)(2,1)S(1)}, u32[]{:S(2)}, u32[]{:S(2)}) collective-permute-start(bf16[64,1024]{1,0:T(8,128)(2,1)S(1)} %copy.17), channel_id=1, source_target_pairs={{0,1},{1,2},{2,3},{3,0},{4,5},{5,6},{6,7},{7,4},{8,9},{9,10},{10,1... | collective-permute-start | bytes 393224 | tf_op jit(solution)/shard_map/while/body/eval_jaxpr/ppermute | solution.py:10
  19.8 2.9 %collective-permute-start.2 = (f32[1024]{0:T(1024)S(1)}, f32[1024]{0:T(1024)S(1)}, u32[]{:S(2)}, u32[]{:S(2)}) collective-permute-start(f32[1024]{0:T(1024)S(1)} %get-tuple-element.502), channel_id=1, source_target_pairs={{0,1},{1,2},{2,3},{3,0},{4,5},{5,6},{6,7},{7,4},{8,9},{9,10},{10,1... | collective-permute-start | bytes 12296 | tf_op jit(solution)/shard_map/while/body/eval_jaxpr/ppermute | solution.py:10
  22.8 2.4 %collective-permute-done.1 = f32[1024]{0:T(1024)S(1)} collective-permute-done((f32[1024]{0:T(1024)S(1)}, f32[1024]{0:T(1024)S(1)}, u32[]{:S(2)}, u32[]{:S(2)}) %collective-permute-start.1) | collective-permute-done | bytes 4128 | tf_op jit(solution)/shard_map/while/body/eval_jaxpr/ppermute | solution.py:10
  25.3 1.1 %collective-permute-start = (bf16[64,1024]{1,0:T(8,128)(2,1)S(1)}, bf16[64,1024]{1,0:T(8,128)(2,1)S(1)}, u32[]{:S(2)}, u32[]{:S(2)}) collective-permute-start(bf16[64,1024]{1,0:T(8,128)(2,1)S(1)} %copy.17), channel_id=1, source_target_pairs={{0,1},{1,2},{2,3},{3,0},{4,5},{5,6},{6,7},{7,4},{8,9},{9,10},{10,1... | collective-permute-start | bytes 393224 | tf_op jit(solution)/shard_map/while/body/eval_jaxpr/ppermute | solution.py:10
  27.5 0.5 collective-permute-start.1
  28.0 1.6 %collective-permute-start.2 = (f32[1024]{0:T(1024)S(1)}, f32[1024]{0:T(1024)S(1)}, u32[]{:S(2)}, u32[]{:S(2)}) collective-permute-start(f32[1024]{0:T(1024)S(1)} %get-tuple-element.502), channel_id=1, source_target_pairs={{0,1},{1,2},{2,3},{3,0},{4,5},{5,6},{6,7},{7,4},{8,9},{9,10},{10,1... | collective-permute-start | bytes 12296 | tf_op jit(solution)/shard_map/while/body/eval_jaxpr/ppermute | solution.py:10
  29.6 3.4 %collective-permute-done.1 = f32[1024]{0:T(1024)S(1)} collective-permute-done((f32[1024]{0:T(1024)S(1)}, f32[1024]{0:T(1024)S(1)}, u32[]{:S(2)}, u32[]{:S(2)}) %collective-permute-start.1) | collective-permute-done | bytes 4128 | tf_op jit(solution)/shard_map/while/body/eval_jaxpr/ppermute | solution.py:10
  34.6 1.6 %collective-permute-start.1 = (f32[1024]{0:T(1024)S(1)}, f32[1024]{0:T(1024)S(1)}, u32[]{:S(2)}, u32[]{:S(2)}) collective-permute-start(f32[1024]{0:T(1024)S(1)} %get-tuple-element.501), channel_id=1, source_target_pairs={{0,1},{1,2},{2,3},{3,0},{4,5},{5,6},{6,7},{7,4},{8,9},{9,10},{10,1... | collective-permute-start | bytes 12296 | tf_op jit(solution)/shard_map/while/body/eval_jaxpr/ppermute | solution.py:10
  36.2 1.1 %collective-permute-start.2 = (f32[1024]{0:T(1024)S(1)}, f32[1024]{0:T(1024)S(1)}, u32[]{:S(2)}, u32[]{:S(2)}) collective-permute-start(f32[1024]{0:T(1024)S(1)} %get-tuple-element.502), channel_id=1, source_target_pairs={{0,1},{1,2},{2,3},{3,0},{4,5},{5,6},{6,7},{7,4},{8,9},{9,10},{10,1... | collective-permute-start | bytes 12296 | tf_op jit(solution)/shard_map/while/body/eval_jaxpr/ppermute | solution.py:10
  37.3 3.8 %collective-permute-done.1 = f32[1024]{0:T(1024)S(1)} collective-permute-done((f32[1024]{0:T(1024)S(1)}, f32[1024]{0:T(1024)S(1)}, u32[]{:S(2)}, u32[]{:S(2)}) %collective-permute-start.1) | collective-permute-done | bytes 4128 | tf_op jit(solution)/shard_map/while/body/eval_jaxpr/ppermute | solution.py:10
  41.1 0.5 collective-permute-done.2
  41.8 0.5 subtract_reduce_fusion.3
  42.8 1.6 %collective-permute-start.1 = (f32[1024]{0:T(1024)S(1)}, f32[1024]{0:T(1024)S(1)}, u32[]{:S(2)}, u32[]{:S(2)}) collective-permute-start(f32[1024]{0:T(1024)S(1)} %get-tuple-element.501), channel_id=1, source_target_pairs={{0,1},{1,2},{2,3},{3,0},{4,5},{5,6},{6,7},{7,4},{8,9},{9,10},{10,1... | collective-permute-start | bytes 12296 | tf_op jit(solution)/shard_map/while/body/eval_jaxpr/ppermute | solution.py:10
  44.4 4.1 %collective-permute-done.1 = f32[1024]{0:T(1024)S(1)} collective-permute-done((f32[1024]{0:T(1024)S(1)}, f32[1024]{0:T(1024)S(1)}, u32[]{:S(2)}, u32[]{:S(2)}) %collective-permute-start.1) | collective-permute-done | bytes 4128 | tf_op jit(solution)/shard_map/while/body/eval_jaxpr/ppermute | solution.py:10
  48.5 1.2 %collective-permute-done.2 = f32[1024]{0:T(1024)S(1)} collective-permute-done((f32[1024]{0:T(1024)S(1)}, f32[1024]{0:T(1024)S(1)}, u32[]{:S(2)}, u32[]{:S(2)}) %collective-permute-start.2) | collective-permute-done | bytes 4128 | tf_op jit(solution)/shard_map/while/body/eval_jaxpr/ppermute | solution.py:10
  49.7 5.2 %all-gather = f32[4096]{0:T(1024)S(1)} all-gather(f32[1024]{0:T(1024)S(1)} %get-tuple-element.300), channel_id=2, replica_groups=mesh['pair'=2,'rep'=4,'blk'=4] {'rep'}, dimensions={0}, use_global_device_ids=true | all-gather | bytes 20480 | tf_op jit(solution)/shard_map/all_gather | solution.py:14
  54.9 5.2 %all-gather.1 = f32[4096]{0:T(1024)S(1)} all-gather(f32[1024]{0:T(1024)S(1)} %get-tuple-element.301), channel_id=3, replica_groups=mesh['pair'=2,'rep'=4,'blk'=4] {'rep'}, dimensions={0}, use_global_device_ids=true | all-gather | bytes 20480 | tf_op jit(solution)/shard_map/all_gather | solution.py:14
  60.2 0.7 %slice-done = f32[1024]{0:T(1024)S(1)} async-done(((f32[4096]{0:T(1024)}), f32[1024]{0:T(1024)S(1)}, s32[]{:S(2)}) %slice-start) | async-done | bytes 4120 | tf_op jit(solution)/shard_map/slice | solution.py:15
  61.0 0.6 add_multiply_fusion
  61.6 0.6 add_multiply_fusion.1
  (82 shorter events, 4.7 us)
Async XLA Ops:
  0.6 16.4 %copy-start = (bf16[64,1024]{1,0:T(8,128)(2,1)S(1)}, bf16[64,1024]{1,0:T(8,128)(2,1)}, u32[]{:S(2)}) copy-start(bf16[64,1024]{1,0:T(8,128)(2,1)} %param.11) | copy-start | bytes 393220
  0.6 0.7 %copy-start.3 = (f32[1024]{0:T(1024)S(1)}, f32[1024]{0:T(1024)}, u32[]{:S(2)}) copy-start(f32[1024]{0:T(1024)} %param.15) | copy-start | bytes 12292
  0.7 0.7 %copy-start.4 = (f32[1024]{0:T(1024)S(1)}, f32[1024]{0:T(1024)}, u32[]{:S(2)}) copy-start(f32[1024]{0:T(1024)} %param.13) | copy-start | bytes 12292
  0.7 15.6 %copy-start.2 = (bf16[64,256]{1,0:T(8,128)(2,1)S(1)}, bf16[64,256]{1,0:T(8,128)(2,1)}, u32[]{:S(2)}) copy-start(bf16[64,256]{1,0:T(8,128)(2,1)} %param.10) | copy-start | bytes 98308
  16.3 0.7 %copy-start.6 = (f32[256]{0:T(256)S(1)}, f32[256]{0:T(256)}, u32[]{:S(2)}) copy-start(f32[256]{0:T(256)} %param.12) | copy-start | bytes 3076
  16.3 0.7 %copy-start.5 = (f32[256]{0:T(256)S(1)}, f32[256]{0:T(256)}, u32[]{:S(2)}) copy-start(f32[256]{0:T(256)} %param.14) | copy-start | bytes 3076
  17.1 8.2 %collective-permute-start = (bf16[64,1024]{1,0:T(8,128)(2,1)S(1)}, bf16[64,1024]{1,0:T(8,128)(2,1)S(1)}, u32[]{:S(2)}, u32[]{:S(2)}) collective-permute-start(bf16[64,1024]{1,0:T(8,128)(2,1)S(1)} %copy.17), channel_id=1, source_target_pairs={{0,1},{1,2},{2,3},{3,0},{4,5},{5,6},{6,7},{7,4},{8,9},{9,10},{10,1... | collective-permute-start | bytes 393224 | tf_op jit(solution)/shard_map/while/body/eval_jaxpr/ppermute | solution.py:10
  19.8 5.5 %collective-permute-start.1 = (f32[1024]{0:T(1024)S(1)}, f32[1024]{0:T(1024)S(1)}, u32[]{:S(2)}, u32[]{:S(2)}) collective-permute-start(f32[1024]{0:T(1024)S(1)} %get-tuple-element.501), channel_id=1, source_target_pairs={{0,1},{1,2},{2,3},{3,0},{4,5},{5,6},{6,7},{7,4},{8,9},{9,10},{10,1... | collective-permute-start | bytes 12296 | tf_op jit(solution)/shard_map/while/body/eval_jaxpr/ppermute | solution.py:10
  19.8 5.5 %collective-permute-start.2 = (f32[1024]{0:T(1024)S(1)}, f32[1024]{0:T(1024)S(1)}, u32[]{:S(2)}, u32[]{:S(2)}) collective-permute-start(f32[1024]{0:T(1024)S(1)} %get-tuple-element.502), channel_id=1, source_target_pairs={{0,1},{1,2},{2,3},{3,0},{4,5},{5,6},{6,7},{7,4},{8,9},{9,10},{10,1... | collective-permute-start | bytes 12296 | tf_op jit(solution)/shard_map/while/body/eval_jaxpr/ppermute | solution.py:10
  25.3 8.1 %collective-permute-start = (bf16[64,1024]{1,0:T(8,128)(2,1)S(1)}, bf16[64,1024]{1,0:T(8,128)(2,1)S(1)}, u32[]{:S(2)}, u32[]{:S(2)}) collective-permute-start(bf16[64,1024]{1,0:T(8,128)(2,1)S(1)} %copy.17), channel_id=1, source_target_pairs={{0,1},{1,2},{2,3},{3,0},{4,5},{5,6},{6,7},{7,4},{8,9},{9,10},{10,1... | collective-permute-start | bytes 393224 | tf_op jit(solution)/shard_map/while/body/eval_jaxpr/ppermute | solution.py:10
  27.5 5.5 %collective-permute-start.1 = (f32[1024]{0:T(1024)S(1)}, f32[1024]{0:T(1024)S(1)}, u32[]{:S(2)}, u32[]{:S(2)}) collective-permute-start(f32[1024]{0:T(1024)S(1)} %get-tuple-element.501), channel_id=1, source_target_pairs={{0,1},{1,2},{2,3},{3,0},{4,5},{5,6},{6,7},{7,4},{8,9},{9,10},{10,1... | collective-permute-start | bytes 12296 | tf_op jit(solution)/shard_map/while/body/eval_jaxpr/ppermute | solution.py:10
  28.0 5.4 %collective-permute-start.2 = (f32[1024]{0:T(1024)S(1)}, f32[1024]{0:T(1024)S(1)}, u32[]{:S(2)}, u32[]{:S(2)}) collective-permute-start(f32[1024]{0:T(1024)S(1)} %get-tuple-element.502), channel_id=1, source_target_pairs={{0,1},{1,2},{2,3},{3,0},{4,5},{5,6},{6,7},{7,4},{8,9},{9,10},{10,1... | collective-permute-start | bytes 12296 | tf_op jit(solution)/shard_map/while/body/eval_jaxpr/ppermute | solution.py:10
  33.4 8.2 %collective-permute-start = (bf16[64,1024]{1,0:T(8,128)(2,1)S(1)}, bf16[64,1024]{1,0:T(8,128)(2,1)S(1)}, u32[]{:S(2)}, u32[]{:S(2)}) collective-permute-start(bf16[64,1024]{1,0:T(8,128)(2,1)S(1)} %copy.17), channel_id=1, source_target_pairs={{0,1},{1,2},{2,3},{3,0},{4,5},{5,6},{6,7},{7,4},{8,9},{9,10},{10,1... | collective-permute-start | bytes 393224 | tf_op jit(solution)/shard_map/while/body/eval_jaxpr/ppermute | solution.py:10
  34.6 6.5 %collective-permute-start.1 = (f32[1024]{0:T(1024)S(1)}, f32[1024]{0:T(1024)S(1)}, u32[]{:S(2)}, u32[]{:S(2)}) collective-permute-start(f32[1024]{0:T(1024)S(1)} %get-tuple-element.501), channel_id=1, source_target_pairs={{0,1},{1,2},{2,3},{3,0},{4,5},{5,6},{6,7},{7,4},{8,9},{9,10},{10,1... | collective-permute-start | bytes 12296 | tf_op jit(solution)/shard_map/while/body/eval_jaxpr/ppermute | solution.py:10
  36.2 5.4 %collective-permute-start.2 = (f32[1024]{0:T(1024)S(1)}, f32[1024]{0:T(1024)S(1)}, u32[]{:S(2)}, u32[]{:S(2)}) collective-permute-start(f32[1024]{0:T(1024)S(1)} %get-tuple-element.502), channel_id=1, source_target_pairs={{0,1},{1,2},{2,3},{3,0},{4,5},{5,6},{6,7},{7,4},{8,9},{9,10},{10,1... | collective-permute-start | bytes 12296 | tf_op jit(solution)/shard_map/while/body/eval_jaxpr/ppermute | solution.py:10
  41.6 8.1 %collective-permute-start = (bf16[64,1024]{1,0:T(8,128)(2,1)S(1)}, bf16[64,1024]{1,0:T(8,128)(2,1)S(1)}, u32[]{:S(2)}, u32[]{:S(2)}) collective-permute-start(bf16[64,1024]{1,0:T(8,128)(2,1)S(1)} %copy.17), channel_id=1, source_target_pairs={{0,1},{1,2},{2,3},{3,0},{4,5},{5,6},{6,7},{7,4},{8,9},{9,10},{10,1... | collective-permute-start | bytes 393224 | tf_op jit(solution)/shard_map/while/body/eval_jaxpr/ppermute | solution.py:10
  42.8 5.7 %collective-permute-start.1 = (f32[1024]{0:T(1024)S(1)}, f32[1024]{0:T(1024)S(1)}, u32[]{:S(2)}, u32[]{:S(2)}) collective-permute-start(f32[1024]{0:T(1024)S(1)} %get-tuple-element.501), channel_id=1, source_target_pairs={{0,1},{1,2},{2,3},{3,0},{4,5},{5,6},{6,7},{7,4},{8,9},{9,10},{10,1... | collective-permute-start | bytes 12296 | tf_op jit(solution)/shard_map/while/body/eval_jaxpr/ppermute | solution.py:10
  44.3 5.4 %collective-permute-start.2 = (f32[1024]{0:T(1024)S(1)}, f32[1024]{0:T(1024)S(1)}, u32[]{:S(2)}, u32[]{:S(2)}) collective-permute-start(f32[1024]{0:T(1024)S(1)} %get-tuple-element.502), channel_id=1, source_target_pairs={{0,1},{1,2},{2,3},{3,0},{4,5},{5,6},{6,7},{7,4},{8,9},{9,10},{10,1... | collective-permute-start | bytes 12296 | tf_op jit(solution)/shard_map/while/body/eval_jaxpr/ppermute | solution.py:10
  54.9 5.2 %copy-start.1 = (f32[4096]{0:T(1024)}, f32[4096]{0:T(1024)S(1)}, u32[]{:S(2)}) copy-start(f32[4096]{0:T(1024)S(1)} %all-gather) | copy-start | bytes 49156
  60.2 0.7 %slice-start = ((f32[4096]{0:T(1024)}), f32[1024]{0:T(1024)S(1)}, s32[]{:S(2)}) async-start(f32[4096]{0:T(1024)} %copy-done.1), calls=%async_computation | async-start | bytes 8192 | tf_op jit(solution)/shard_map/slice | solution.py:15
where the time goes:
time: 62.4 us; the launch traced here: 62.2 us
  blocking collectives  25.3 us (41%)
  waiting for transfers between devices  16 us (26%)
  starting transfers between devices  12.2 us (20%)
  other arithmetic  3.3 us (5%)
  local copies, waits for them, and re-layouts  2.21 us (4%)
  matrix products  1.93 us (3%)
  between operations  0.73 us (1%)
    ppermute x12, waiting for transfers between devices, passed_along(): return lax.ppermute(value, axis, pairs)  16 us
    all_gather x1, blocking collectives, on_device(): lax.all_gather(log_tgt_weight + tgt_potential, 'blk', axis=0, tiled=True)  14.9 us
    ppermute x12, starting transfers between devices, passed_along(): return lax.ppermute(value, axis, pairs)  12.2 us
    all_gather x2, blocking collectives, merged(): pieces = jax.tree.map(lambda part: lax.all_gather(part, axis), value)  10.4 us
    dot_general x4, matrix products, tile_scores(): lax.dot_general(src_spectra, spectra_piece, (((0,), (0,)), ((), ())), pre...  1.93 us
    reduce_sum x4, other arithmetic, column_part(): jnp.sum(jnp.exp(col_scores - block_peak[None, :]), axis=0)  1.74 us
    unnamed x14, local copies, waits for them, and re-layouts  1.4 us
  transfers between devices with their start and end apart: 12, of which 8 were waited for; matrix products, arithmetic and copies ran while one was open for 6% of the time, Pallas kernels for 0%

commit v1 on v0

v1 whole, which is shorter than its diff:
```python
import functools

import jax
import jax.numpy as jnp
from jax import lax
from jax.experimental import pallas as pl
from jax.experimental.pallas import tpu as pltpu
from jax.sharding import PartitionSpec as P

EXTRA = 8


def partners(axis):
    count = lax.axis_size(axis)
    if count & (count - 1) == 0:
        return [[(i, i ^ s) for i in range(count)] for s in range(count - 1, 0, -1)]
    return [[(i, (i + s) % count) for i in range(count)] for s in range(1, count)]


def back(pattern):
    return [(target, source) for source, target in pattern]


def three_parts(value):
    high = value.astype(jnp.bfloat16).astype(jnp.float32)
    rest = value - high
    middle = rest.astype(jnp.bfloat16).astype(jnp.float32)
    low = (rest - middle).astype(jnp.bfloat16).astype(jnp.float32)
    return high, middle, low


def extra_rows(width, rows):
    index = lax.broadcasted_iota(jnp.int32, (EXTRA, width), 0)
    block = jnp.zeros((EXTRA, width), jnp.float32)
    for at, row in rows.items():
        block = jnp.where(index == at, row, block)
    return block.astype(jnp.bfloat16)


def half_square(spectra):
    wide = spectra.astype(jnp.float32)
    return 0.5 * jnp.sum(wide * wide, axis=0, keepdims=True)


def pack_kernel(spectra_ref, weight_ref, potential_ref, packed_ref):
    bands, width = spectra_ref.shape
    spectra = spectra_ref[...]
    bias = weight_ref[...] + potential_ref[...] - half_square(spectra)
    high, middle, low = three_parts(bias)
    packed_ref[:bands, :] = spectra
    packed_ref[bands:, :] = extra_rows(
        width, {0: high, 1: middle, 2: low, 3: 1.0, 4: 1.0, 5: 1.0}
    )


def log_sum(scores):
    peak = jnp.max(scores, axis=0, keepdims=True)
    return peak, jnp.sum(jnp.exp(scores - peak), axis=0, keepdims=True)


def tile_stats(packed, turned, col_operand):
    row_scores = jnp.dot(turned, packed, preferred_element_type=jnp.float32)
    row_peak, row_total = log_sum(row_scores)
    col_scores = lax.dot_general(
        packed, col_operand, (((0,), (0,)), ((), ())), preferred_element_type=jnp.float32
    )
    return row_peak + jnp.log(row_total), log_sum(col_scores)


def merge_parts(parts):
    peak = functools.reduce(jnp.maximum, [part[0] for part in parts])
    return peak, sum(part[1] * jnp.exp(part[0] - peak) for part in parts)


def home_kernel(
    packed_ref, spectra_ref, weight_ref, potential_ref, src_spectra_ref, src_potential_ref,
    turned_ref, operand_ref, rows_ref, col_peak_ref, col_total_ref, src_base_ref, tgt_base_ref,
):
    bands, width = spectra_ref.shape
    spectra = spectra_ref[...]
    square = half_square(spectra)
    high, middle, low = three_parts(weight_ref[...] + potential_ref[...] - square)
    row_operand = jnp.concatenate(
        [spectra, extra_rows(width, {3: high, 4: middle, 5: low})], axis=0
    )
    turned_ref[...] = row_operand.T
    operand_ref[:bands, :] = spectra
    operand_ref[bands:, :] = extra_rows(width, {0: 1.0, 1: 1.0, 2: 1.0})
    rows, (peak, total) = tile_stats(packed_ref[...], turned_ref[...], operand_ref[...])
    rows_ref[...] = rows
    col_peak_ref[...] = peak
    col_total_ref[...] = total
    src_base_ref[...] = src_potential_ref[...] + half_square(src_spectra_ref[...])
    tgt_base_ref[...] = potential_ref[...] + square


def away_kernel(turned_ref, operand_ref, col_peak_ref, col_total_ref, *refs):
    count = (len(refs) - 1) // 2
    parts = [(col_peak_ref[...], col_total_ref[...])]
    for packed_ref, rows_ref in zip(refs[:count], refs[count : 2 * count]):
        rows, part = tile_stats(packed_ref[...], turned_ref[...], operand_ref[...])
        rows_ref[...] = rows
        parts.append(part)
    peak, total = merge_parts(parts)
    refs[-1][...] = peak + jnp.log(total)


def joined_logs(logs):
    peak = functools.reduce(jnp.maximum, logs)
    return peak + jnp.log(sum(jnp.exp(log - peak) for log in logs))


def final_kernel(rows_count, src_base_ref, tgt_base_ref, *refs):
    logs, (src_ref, tgt_ref) = [ref[...] for ref in refs[:-2]], refs[-2:]
    src_ref[...] = 0.5 * (src_base_ref[...] - joined_logs(logs[:rows_count]))
    tgt_ref[...] = 0.5 * (tgt_base_ref[...] - joined_logs(logs[rows_count:]))


def cost(flops):
    return pl.CostEstimate(flops=flops, bytes_accessed=1 << 18, transcendentals=1 << 18)


def on_device(
    src_spectra, tgt_spectra, log_src_weight, log_tgt_weight, src_potential, tgt_potential
):
    bands, rows = src_spectra.shape
    columns = tgt_spectra.shape[1]
    depth = bands + EXTRA
    f32 = functools.partial(jax.ShapeDtypeStruct, dtype=jnp.float32)
    bf16 = functools.partial(jax.ShapeDtypeStruct, dtype=jnp.bfloat16)
    flat = lambda value: value.reshape(1, -1)
    tile_flops = 4 * rows * columns * depth

    packed = pl.pallas_call(pack_kernel, out_shape=bf16((depth, rows)))(
        src_spectra, flat(log_src_weight), flat(src_potential)
    )
    patterns = partners("blk")
    arrived = [lax.ppermute(packed, "blk", pattern) for pattern in patterns]
    turned, operand, home_rows, peak, total, src_base, tgt_base = pl.pallas_call(
        home_kernel,
        out_shape=(
            bf16((columns, depth)), bf16((depth, columns)), f32((1, rows)),
            f32((1, columns)), f32((1, columns)), f32((1, rows)), f32((1, columns)),
        ),
        cost_estimate=cost(tile_flops),
    )(packed, tgt_spectra, flat(log_tgt_weight), flat(tgt_potential), src_spectra, flat(src_potential))
    *away_rows, col_logs = pl.pallas_call(
        away_kernel,
        out_shape=tuple(f32((1, rows)) for _ in arrived) + (f32((1, columns)),),
        cost_estimate=cost(tile_flops * max(1, len(arrived))),
    )(turned, operand, peak, total, *arrived)
    row_logs = [home_rows] + [
        lax.ppermute(value, "blk", back(pattern)) for value, pattern in zip(away_rows, patterns)
    ]
    copies = lax.axis_size("rep")
    if copies & (copies - 1) == 0:
        last = [col_logs]
        step = 1
        while step < copies:
            held = last[0] if len(last) == 1 else joined_logs(last)
            last = [held, lax.ppermute(held, "rep", [(i, i ^ step) for i in range(copies)])]
            step *= 2
    else:
        last = [col_logs] + [lax.ppermute(col_logs, "rep", p) for p in partners("rep")]
    src_updated, tgt_updated = pl.pallas_call(
        functools.partial(final_kernel, len(row_logs)),
        out_shape=(f32((1, rows)), f32((1, columns))),
    )(src_base, tgt_base, *row_logs, *last)
    return src_updated.reshape(-1), tgt_updated.reshape(-1)


def solution(mesh):
    placed = (
        P(None, ("pair", "rep", "blk")),
        P(None, ("pair", "blk")),
        P(("pair", "rep", "blk")),
        P(("pair", "blk")),
        P(("pair", "rep", "blk")),
        P(("pair", "blk")),
    )
    return jax.shard_map(
        on_device,
        mesh=mesh,
        in_specs=placed,
        out_specs=(P(("pair", "rep", "blk")), P(("pair", "blk"))),
        check_vma=False,
    )
```

time: 62.4 us -> 29.4 us (0.47)
  blocking collectives: 25.3 us -> 0 us
  waiting for transfers between devices: 16 us -> 6.58 us
  Pallas kernels: 0 us -> 8.34 us
  other arithmetic: 3.3 us -> 0.7 us
  matrix products: 1.93 us -> 0 us
  starting transfers between devices: 12.2 us -> 10.8 us
    all_gather x3 -> x0, blocking collectives: 25.3 us -> none  [the longest x1 14.9 us: on_device(): lax.all_gather(log_tgt_weight + tgt_potential, 'blk', axis=0, tiled=True)]
    ppermute x12 -> x8, waiting for transfers between devices: 16 us -> 6.58 us  [the longest x3 3.65 us: on_device(): arrived = [lax.ppermute(packed, 'blk', pattern) for pattern in patterns]]
    pallas_call x0 -> x4, Pallas kernels: none -> 8.34 us  [the longest x1 3.29 us: on_device(): pl.pallas_call(away_kernel, out_shape=tuple((f32((1, rows)) for _ in arri...]
    dot_general x4 -> x0, matrix products: 1.93 us -> none  [tile_scores(): lax.dot_general(src_spectra, spectra_piece, (((0,), (0,)), ((), ())), pre...]
    reduce_sum x9 -> x0, other arithmetic: 1.93 us -> none  [the longest x4 1.74 us: column_part(): jnp.sum(jnp.exp(col_scores - block_peak[None, :]), axis=0)]
    ppermute x12 -> x8, starting transfers between devices: 12.2 us -> 10.8 us  [the longest x3 5.64 us: on_device(): arrived = [lax.ppermute(packed, 'blk', pattern) for pattern in patterns]]
    mul x7 -> x0, other arithmetic: 1.2 us -> none  [the longest x2 1.18 us: on_device(): return (0.5 * (src_potential + src_new), 0.5 * (tgt_potential + tgt_new))]
    slice x7 -> x0, local copies, waits for them, and re-layouts: 0.69 us -> none  [the longest x3 0.66 us: merged(): head = jax.tree.map(lambda part: part[0], pieces)]
  transfers between devices with their start and end apart: 12 -> 8, of which waited for: 8 -> 5; matrix products, arithmetic and copies ran while one was open for 6% -> 0% of each run, Pallas kernels for 0% -> 8%
where the time goes in v1:
time: 29.4 us; the launch traced here: 29.1 us
  starting transfers between devices  10.8 us (37%)
  Pallas kernels  8.34 us (28%)
  waiting for transfers between devices  6.58 us (22%)
  local copies, waits for them, and re-layouts  2.04 us (7%)
  other arithmetic  0.7 us (2%)
  between operations  0.7 us (2%)
    ppermute x3, starting transfers between devices, on_device(): arrived = [lax.ppermute(packed, 'blk', pattern) for pattern in patterns]  5.64 us
    ppermute x3, waiting for transfers between devices, on_device(): arrived = [lax.ppermute(packed, 'blk', pattern) for pattern in patterns]  3.65 us
    ppermute x3, starting transfers between devices, on_device(): lax.ppermute(value, 'blk', back(pattern))  3.55 us
    pallas_call x1, Pallas kernels, on_device(): pl.pallas_call(away_kernel, out_shape=tuple((f32((1, rows)) for _ in arri...  3.29 us
    pallas_call x1, Pallas kernels, on_device(): pl.pallas_call(home_kernel, out_shape=(bf16((columns, depth)), bf16((dept...  2.29 us
    unnamed x22, local copies, waits for them, and re-layouts  2.04 us
    ppermute x2, starting transfers between devices, on_device(): lax.ppermute(held, 'rep', [(i, i ^ step) for i in range(copies)])  1.56 us
    ppermute x3, waiting for transfers between devices, on_device(): lax.ppermute(value, 'blk', back(pattern))  1.55 us
  transfers between devices with their start and end apart: 8, of which 5 were waited for; matrix products, arithmetic and copies ran while one was open for 0% of the time, Pallas kernels for 8%

profile of v1, /device:TPU:0, one launch (start us, length us, event | category | flops | bytes accessed | tf_op | source)
XLA Modules:
  0.0 29.1 jit_solution(16026996364917512627)
XLA Ops:
  0.6 1.4 %shard_map.77.packed_ref = bf16[72,256]{1,0:T(8,128)(2,1)} custom-call(bf16[64,256]{1,0:T(8,128)(2,1)} %src_spectra_ref.1, f32[1,256]{1,0:T(1,128)} %bitcast.6, f32[1,256]{1,0:T(1,128)} %bitcast.7), custom_call_target="tpu_custom_call" | custom-call | tf_op jit(solution)/shard_map/pallas_call | solution.py:134
  2.1 3.1 %collective-permute-start.2 = (bf16[72,256]{1,0:T(8,128)(2,1)}, bf16[72,256]{1,0:T(8,128)(2,1)S(1)}, u32[]{:S(2)}, u32[]{:S(2)}) collective-permute-start(bf16[72,256]{1,0:T(8,128)(2,1)} %shard_map.77.packed_ref), channel_id=1, source_target_pairs={{0,1},{1,0},{2,3},{3,2},{4,5},{5,4},{6,7},{7,6},{8,9},{9,8},{10,11... | collective-permute-start | bytes 110600 | tf_op jit(solution)/shard_map/ppermute | solution.py:138
  5.1 2.6 %collective-permute-start.1 = (bf16[72,256]{1,0:T(8,128)(2,1)}, bf16[72,256]{1,0:T(8,128)(2,1)S(1)}, u32[]{:S(2)}, u32[]{:S(2)}) collective-permute-start(bf16[72,256]{1,0:T(8,128)(2,1)} %shard_map.77.packed_ref), channel_id=1, source_target_pairs={{0,2},{1,3},{2,0},{3,1},{4,6},{5,7},{6,4},{7,5},{8,10},{9,11},{10,... | collective-permute-start | bytes 110600 | tf_op jit(solution)/shard_map/ppermute | solution.py:138
  7.7 0.0 collective-permute-start
  7.7 2.3 %shard_map.78 = (bf16[1024,72]{1,0:T(8,128)(2,1)}, bf16[72,1024]{1,0:T(8,128)(2,1)}, f32[1,256]{1,0:T(1,128)}, f32[1,1024]{1,0:T(1,128)}, f32[1,1024]{1,0:T(1,12...) custom-call(bf16[72,256]{1,0:T(8,128)(2,1)} %shard_map.77.packed_ref, bf16[64,1024]{1,0:T(8,128)(2,1)} %spectra_ref.3, ...), custom_call_target="tpu_custom_call" | custom-call | flops 75497472 | bytes 262144 | tf_op jit(solution)/shard_map/pallas_call | solution.py:139
  10.0 0.0 collective-permute-done.2.refs_2_
  10.0 0.8 %collective-permute-done.1.refs_1_ = bf16[72,256]{1,0:T(8,128)(2,1)S(1)} collective-permute-done((bf16[72,256]{1,0:T(8,128)(2,1)}, bf16[72,256]{1,0:T(8,128)(2,1)S(1)}, u32[]{:S(2)}, u32[]{:S(2)}) %collective-permute-start.1) | collective-permute-done | bytes 36896 | tf_op jit(solution)/shard_map/ppermute | solution.py:138
  10.9 2.8 %collective-permute-done.refs_0_ = bf16[72,256]{1,0:T(8,128)(2,1)S(1)} collective-permute-done((bf16[72,256]{1,0:T(8,128)(2,1)}, bf16[72,256]{1,0:T(8,128)(2,1)S(1)}, u32[]{:S(2)}, u32[]{:S(2)}) %collective-permute-start) | collective-permute-done | bytes 36896 | tf_op jit(solution)/shard_map/ppermute | solution.py:138
  13.7 0.6 %copy-done.7 = bf16[72,256]{1,0:T(8,128)(2,1)} copy-done((bf16[72,256]{1,0:T(8,128)(2,1)}, bf16[72,256]{1,0:T(8,128)(2,1)S(1)}, u32[]{:S(2)}) %copy-start.7) | copy-done | bytes 36888
  14.3 3.3 %shard_map.79 = (f32[1,256]{1,0:T(1,128)}, f32[1,256]{1,0:T(1,128)}, f32[1,256]{1,0:T(1,128)}, f32[1,1024]{1,0:T(1,128)}) custom-call(bf16[1024,72]{1,0:T(8,128)(2,1)} %get-tuple-element.18.turned_ref, bf16[72,1024]{1,0:T(8,128)(2,1)} %get-tuple-element.19.operand_ref, f32[1,1024]{1,0:T(1,128)} %get-tuple-element.20.col_peak_ref, ...), custom_call_target="tpu_custom_call" | custom-call | flops 226492416 | bytes 262144 | tf_op jit(solution)/shard_map/pallas_call | solution.py:147
  17.6 1.4 %collective-permute-done.6 = f32[1,1024]{1,0:T(1,128)S(1)} collective-permute-done((f32[1,1024]{1,0:T(1,128)}, f32[1,1024]{1,0:T(1,128)S(1)}, u32[]{:S(2)}, u32[]{:S(2)}) %collective-permute-start.6) | collective-permute-done | bytes 4128 | tf_op jit(solution)/shard_map/ppermute | solution.py:161
  19.0 0.7 %log_add_fusion.refs_4_ = f32[1,1024]{1,0:T(1,128)S(1)} fusion(f32[1,1024]{1,0:T(1,128)S(1)} %collective-permute-done.6, f32[1,1024]{1,0:T(1,128)} %get-tuple-element.25), kind=kLoop, calls=%fused_computation | loop fusion | flops 5120 | bytes 12288 | tf_op jit(solution)/shard_map/add | solution.py:110
  19.7 0.0 copy-start.10
  19.7 1.6 %collective-permute-start.7 = (f32[1,1024]{1,0:T(1,128)S(1)}, f32[1,1024]{1,0:T(1,128)S(1)}, u32[]{:S(2)}, u32[]{:S(2)}) collective-permute-start(f32[1,1024]{1,0:T(1,128)S(1)} %log_add_fusion.refs_4_), channel_id=1, source_target_pairs={{0,8},{4,12},{8,0},{12,4},{1,9},{5,13},{9,1},{13,5},{2,10},{6,14},... | collective-permute-start | bytes 12296 | tf_op jit(solution)/shard_map/ppermute | solution.py:161
  21.2 0.5 %collective-permute-start.3 = (f32[1,256]{1,0:T(1,128)S(1)}, f32[1,256]{1,0:T(1,128)S(1)}, u32[]{:S(2)}, u32[]{:S(2)}) collective-permute-start(f32[1,256]{1,0:T(1,128)S(1)} %copy-done.10), channel_id=1, source_target_pairs={{3,0},{2,1},{1,2},{0,3},{7,4},{6,5},{5,6},{4,7},{11,8},{10,9},{9,1... | collective-permute-start | bytes 3080 | tf_op jit(solution)/shard_map/ppermute | solution.py:153
  21.7 0.2 copy-done.9
  21.9 0.0 collective-permute-start.4
  21.9 0.7 %copy-done.8 = f32[1,256]{1,0:T(1,128)S(1)} copy-done((f32[1,256]{1,0:T(1,128)S(1)}, f32[1,256]{1,0:T(1,128)}, u32[]{:S(2)}) %copy-start.8) | copy-done | bytes 1048
  22.6 3.1 %collective-permute-start.5 = (f32[1,256]{1,0:T(1,128)S(1)}, f32[1,256]{1,0:T(1,128)S(1)}, u32[]{:S(2)}, u32[]{:S(2)}) collective-permute-start(f32[1,256]{1,0:T(1,128)S(1)} %copy-done.8), channel_id=1, source_target_pairs={{1,0},{0,1},{3,2},{2,3},{5,4},{4,5},{7,6},{6,7},{9,8},{8,9},{11,10... | collective-permute-start | bytes 3080 | tf_op jit(solution)/shard_map/ppermute | solution.py:153
  25.6 1.0 %collective-permute-done.3.refs_1_ = f32[1,256]{1,0:T(1,128)S(1)} collective-permute-done((f32[1,256]{1,0:T(1,128)S(1)}, f32[1,256]{1,0:T(1,128)S(1)}, u32[]{:S(2)}, u32[]{:S(2)}) %collective-permute-start.3) | collective-permute-done | bytes 1056 | tf_op jit(solution)/shard_map/ppermute | solution.py:153
  26.6 0.6 %collective-permute-done.5.refs_3_ = f32[1,256]{1,0:T(1,128)S(1)} collective-permute-done((f32[1,256]{1,0:T(1,128)S(1)}, f32[1,256]{1,0:T(1,128)S(1)}, u32[]{:S(2)}, u32[]{:S(2)}) %collective-permute-start.5) | collective-permute-done | bytes 1056 | tf_op jit(solution)/shard_map/ppermute | solution.py:153
  27.2 0.5 %copy-done.4 = f32[1,256]{1,0:T(1,128)} copy-done((f32[1,256]{1,0:T(1,128)}, f32[1,256]{1,0:T(1,128)S(1)}, u32[]{:S(2)}) %copy-start.4) | copy-done | bytes 1048
  27.8 0.0 copy-done.1
  27.8 1.3 %shard_map.80 = (f32[1,256]{1,0:T(1,128)}, f32[1,1024]{1,0:T(1,128)}) custom-call(f32[1,256]{1,0:T(1,128)} %get-tuple-element.15.src_base_ref, f32[1,1024]{1,0:T(1,128)} %get-tuple-element.16.tgt_base_ref, f32[1,256]{1,0:T(1,128)} %get-tuple-element.17.refs_0_, f32[1,256]{1,0:T(1,128)} %copy-done.2, f32[1,256]{1,0:T(1,128)} %copy-done.3, ...), custom_call_target="tpu_custom_call" | custom-call | tf_op jit(solution)/shard_map/pallas_call | solution.py:165
  (19 shorter events, 0.0 us)
Async XLA Ops:
  2.1 7.9 %collective-permute-start.2 = (bf16[72,256]{1,0:T(8,128)(2,1)}, bf16[72,256]{1,0:T(8,128)(2,1)S(1)}, u32[]{:S(2)}, u32[]{:S(2)}) collective-permute-start(bf16[72,256]{1,0:T(8,128)(2,1)} %shard_map.77.packed_ref), channel_id=1, source_target_pairs={{0,1},{1,0},{2,3},{3,2},{4,5},{5,4},{6,7},{7,6},{8,9},{9,8},{10,11... | collective-permute-start | bytes 110600 | tf_op jit(solution)/shard_map/ppermute | solution.py:138
  5.1 5.7 %collective-permute-start.1 = (bf16[72,256]{1,0:T(8,128)(2,1)}, bf16[72,256]{1,0:T(8,128)(2,1)S(1)}, u32[]{:S(2)}, u32[]{:S(2)}) collective-permute-start(bf16[72,256]{1,0:T(8,128)(2,1)} %shard_map.77.packed_ref), channel_id=1, source_target_pairs={{0,2},{1,3},{2,0},{3,1},{4,6},{5,7},{6,4},{7,5},{8,10},{9,11},{10,... | collective-permute-start | bytes 110600 | tf_op jit(solution)/shard_map/ppermute | solution.py:138
  7.7 6.0 %collective-permute-start = (bf16[72,256]{1,0:T(8,128)(2,1)}, bf16[72,256]{1,0:T(8,128)(2,1)S(1)}, u32[]{:S(2)}, u32[]{:S(2)}) collective-permute-start(bf16[72,256]{1,0:T(8,128)(2,1)} %shard_map.77.packed_ref), channel_id=1, source_target_pairs={{0,3},{1,2},{2,1},{3,0},{4,7},{5,6},{6,5},{7,4},{8,11},{9,10},{10,... | collective-permute-start | bytes 110600 | tf_op jit(solution)/shard_map/ppermute | solution.py:138
  10.0 3.7 %copy-start.5 = (bf16[72,256]{1,0:T(8,128)(2,1)}, bf16[72,256]{1,0:T(8,128)(2,1)S(1)}, u32[]{:S(2)}) copy-start(bf16[72,256]{1,0:T(8,128)(2,1)S(1)} %collective-permute-done.2.refs_2_) | copy-start | bytes 110596
  10.9 2.8 %copy-start.6 = (bf16[72,256]{1,0:T(8,128)(2,1)}, bf16[72,256]{1,0:T(8,128)(2,1)S(1)}, u32[]{:S(2)}) copy-start(bf16[72,256]{1,0:T(8,128)(2,1)S(1)} %collective-permute-done.1.refs_1_) | copy-start | bytes 110596
  13.7 0.6 %copy-start.7 = (bf16[72,256]{1,0:T(8,128)(2,1)}, bf16[72,256]{1,0:T(8,128)(2,1)S(1)}, u32[]{:S(2)}) copy-start(bf16[72,256]{1,0:T(8,128)(2,1)S(1)} %collective-permute-done.refs_0_) | copy-start | bytes 110596
  17.6 1.4 %collective-permute-start.6 = (f32[1,1024]{1,0:T(1,128)}, f32[1,1024]{1,0:T(1,128)S(1)}, u32[]{:S(2)}, u32[]{:S(2)}) collective-permute-start(f32[1,1024]{1,0:T(1,128)} %get-tuple-element.25), channel_id=1, source_target_pairs={{0,4},{4,0},{8,12},{12,8},{1,5},{5,1},{9,13},{13,9},{2,6},{6,2},{1... | collective-permute-start | bytes 12296 | tf_op jit(solution)/shard_map/ppermute | solution.py:161
  19.7 7.5 %copy-start = (f32[1,1024]{1,0:T(1,128)}, f32[1,1024]{1,0:T(1,128)S(1)}, u32[]{:S(2)}) copy-start(f32[1,1024]{1,0:T(1,128)S(1)} %log_add_fusion.refs_4_) | copy-start | bytes 12292
  19.7 1.6 %copy-start.10 = (f32[1,256]{1,0:T(1,128)S(1)}, f32[1,256]{1,0:T(1,128)}, u32[]{:S(2)}) copy-start(f32[1,256]{1,0:T(1,128)} %get-tuple-element.22) | copy-start | bytes 3076
  19.7 7.5 %collective-permute-start.7 = (f32[1,1024]{1,0:T(1,128)S(1)}, f32[1,1024]{1,0:T(1,128)S(1)}, u32[]{:S(2)}, u32[]{:S(2)}) collective-permute-start(f32[1,1024]{1,0:T(1,128)S(1)} %log_add_fusion.refs_4_), channel_id=1, source_target_pairs={{0,8},{4,12},{8,0},{12,4},{1,9},{5,13},{9,1},{13,5},{2,10},{6,14},... | collective-permute-start | bytes 12296 | tf_op jit(solution)/shard_map/ppermute | solution.py:161
  21.2 0.7 %copy-start.9 = (f32[1,256]{1,0:T(1,128)S(1)}, f32[1,256]{1,0:T(1,128)}, u32[]{:S(2)}) copy-start(f32[1,256]{1,0:T(1,128)} %get-tuple-element.23) | copy-start | bytes 3076
  21.2 5.4 %collective-permute-start.3 = (f32[1,256]{1,0:T(1,128)S(1)}, f32[1,256]{1,0:T(1,128)S(1)}, u32[]{:S(2)}, u32[]{:S(2)}) collective-permute-start(f32[1,256]{1,0:T(1,128)S(1)} %copy-done.10), channel_id=1, source_target_pairs={{3,0},{2,1},{1,2},{0,3},{7,4},{6,5},{5,6},{4,7},{11,8},{10,9},{9,1... | collective-permute-start | bytes 3080 | tf_op jit(solution)/shard_map/ppermute | solution.py:153
  21.9 0.7 %copy-start.8 = (f32[1,256]{1,0:T(1,128)S(1)}, f32[1,256]{1,0:T(1,128)}, u32[]{:S(2)}) copy-start(f32[1,256]{1,0:T(1,128)} %get-tuple-element.24) | copy-start | bytes 3076
  21.9 4.7 %collective-permute-start.4 = (f32[1,256]{1,0:T(1,128)S(1)}, f32[1,256]{1,0:T(1,128)S(1)}, u32[]{:S(2)}, u32[]{:S(2)}) collective-permute-start(f32[1,256]{1,0:T(1,128)S(1)} %copy-done.9), channel_id=1, source_target_pairs={{2,0},{3,1},{0,2},{1,3},{6,4},{7,5},{4,6},{5,7},{10,8},{11,9},{8,1... | collective-permute-start | bytes 3080 | tf_op jit(solution)/shard_map/ppermute | solution.py:153
  22.6 4.6 %collective-permute-start.5 = (f32[1,256]{1,0:T(1,128)S(1)}, f32[1,256]{1,0:T(1,128)S(1)}, u32[]{:S(2)}, u32[]{:S(2)}) collective-permute-start(f32[1,256]{1,0:T(1,128)S(1)} %copy-done.8), channel_id=1, source_target_pairs={{1,0},{0,1},{3,2},{2,3},{5,4},{4,5},{7,6},{6,7},{9,8},{8,9},{11,10... | collective-permute-start | bytes 3080 | tf_op jit(solution)/shard_map/ppermute | solution.py:153
  26.6 0.6 %copy-start.2 = (f32[1,256]{1,0:T(1,128)}, f32[1,256]{1,0:T(1,128)S(1)}, u32[]{:S(2)}) copy-start(f32[1,256]{1,0:T(1,128)S(1)} %collective-permute-done.3.refs_1_) | copy-start | bytes 3076
  26.6 0.6 %copy-start.3 = (f32[1,256]{1,0:T(1,128)}, f32[1,256]{1,0:T(1,128)S(1)}, u32[]{:S(2)}) copy-start(f32[1,256]{1,0:T(1,128)S(1)} %collective-permute-done.4.refs_2_) | copy-start | bytes 3076
  27.2 0.6 %copy-start.4 = (f32[1,256]{1,0:T(1,128)}, f32[1,256]{1,0:T(1,128)S(1)}, u32[]{:S(2)}) copy-start(f32[1,256]{1,0:T(1,128)S(1)} %collective-permute-done.5.refs_3_) | copy-start | bytes 3076
  27.2 0.6 %copy-start.1 = (f32[1,1024]{1,0:T(1,128)}, f32[1,1024]{1,0:T(1,128)S(1)}, u32[]{:S(2)}) copy-start(f32[1,1024]{1,0:T(1,128)S(1)} %collective-permute-done.7.refs_5_) | copy-start | bytes 12292

commit v2 on v1

v2 whole, which is shorter than its diff:
```python
import functools

import jax
import jax.numpy as jnp
from jax import lax
from jax.experimental import pallas as pl
from jax.experimental.pallas import tpu as pltpu
from jax.sharding import PartitionSpec as P

EXTRA = 8
PHASE1 = (3, 1, 2)
BASIS = (1, 2)
VMEM = pl.BlockSpec(memory_space=pltpu.VMEM)
HBM = pl.BlockSpec(memory_space=pltpu.HBM)


def three_parts(value):
    high = value.astype(jnp.bfloat16).astype(jnp.float32)
    rest = value - high
    middle = rest.astype(jnp.bfloat16).astype(jnp.float32)
    low = (rest - middle).astype(jnp.bfloat16).astype(jnp.float32)
    return high, middle, low


def extra_rows(width, rows):
    index = lax.broadcasted_iota(jnp.int32, (EXTRA, width), 0)
    block = jnp.zeros((EXTRA, width), jnp.float32)
    for at, row in rows.items():
        block = jnp.where(index == at, row, block)
    return block.astype(jnp.bfloat16)


def half_square(spectra):
    wide = spectra.astype(jnp.float32)
    return 0.5 * jnp.sum(wide * wide, axis=0, keepdims=True)


def pack_kernel(spectra_hbm, weight_hbm, potential_hbm, packed_ref, base_ref, spectra_ref, weight_ref, potential_ref, sems):
    copies = [
        pltpu.make_async_copy(source, target, sems.at[at])
        for at, (source, target) in enumerate(
            ((spectra_hbm, spectra_ref), (weight_hbm, weight_ref), (potential_hbm, potential_ref))
        )
    ]
    for copy in copies:
        copy.start()
    for copy in copies:
        copy.wait()
    bands, width = spectra_ref.shape
    spectra = spectra_ref[...]
    square = half_square(spectra)
    bias = weight_ref[...] + potential_ref[...] - square
    high, middle, low = three_parts(bias)
    packed_ref[:bands, :] = spectra
    packed_ref[bands:, :] = extra_rows(
        width, {0: high, 1: middle, 2: low, 3: 1.0, 4: 1.0, 5: 1.0}
    )
    base_ref[...] = potential_ref[...] + square


def log_sum(blocks):
    peaks, totals = [], []
    for scores in blocks:
        folded = scores.reshape(-1, 8, scores.shape[1])
        peak = jnp.max(folded, axis=0)
        peaks.append(peak)
        totals.append(jnp.sum(jnp.exp(folded - peak[None]), axis=0))
    top = jnp.max(functools.reduce(jnp.maximum, peaks), axis=0, keepdims=True)
    total = sum(total * jnp.exp(peak - top) for peak, total in zip(peaks, totals))
    return top, jnp.sum(total, axis=0, keepdims=True)


def pieces(length, size=256):
    return [slice(at, min(at + size, length)) for at in range(0, length, size)]


def row_logs_of(packed, turned_ref):
    blocks = [
        jnp.dot(turned_ref[piece, :], packed, preferred_element_type=jnp.float32)
        for piece in pieces(turned_ref.shape[0])
    ]
    peak, total = log_sum(blocks)
    return peak + jnp.log(total)


def col_part_of(packed, operand_ref):
    turned = packed.T
    parts = [
        log_sum([jnp.dot(turned, operand_ref[:, piece], preferred_element_type=jnp.float32)])
        for piece in pieces(operand_ref.shape[1], 256)
    ]
    return tuple(jnp.concatenate(part, axis=1) for part in zip(*parts))


def merge_parts(parts):
    peak = functools.reduce(jnp.maximum, [part[0] for part in parts])
    return peak, sum(part[1] * jnp.exp(part[0] - peak) for part in parts)


def home_kernel(
    packed_ref, spectra_ref, weight_ref, potential_ref,
    turned_ref, operand_ref, rows_ref, col_peak_ref, col_total_ref, base_ref,
):
    bands, width = spectra_ref.shape
    spectra = spectra_ref[...]
    square = half_square(spectra)
    high, middle, low = three_parts(weight_ref[...] + potential_ref[...] - square)
    row_operand = jnp.concatenate(
        [spectra, extra_rows(width, {3: high, 4: middle, 5: low})], axis=0
    )
    turned_ref[...] = row_operand.T
    operand_ref[:bands, :] = spectra
    operand_ref[bands:, :] = extra_rows(width, {0: 1.0, 1: 1.0, 2: 1.0})
    packed = packed_ref[...]
    rows_ref[...] = row_logs_of(packed, turned_ref)
    peak, total = col_part_of(packed, operand_ref)
    col_peak_ref[...] = peak
    col_total_ref[...] = total
    base_ref[...] = potential_ref[...] + square


def rows_kernel(packed_ref, turned_ref, *refs):
    fresh = row_logs_of(packed_ref[...], turned_ref)
    refs[-1][0:1, :] = fresh
    for at, ref in enumerate(refs[:-1]):
        refs[-1][at + 1 : at + 2, :] = ref[...]


def give_columns(part, out_refs):
    peak, total = part
    if len(out_refs) == 1:
        out_refs[0][...] = peak + jnp.log(total)
    else:
        out_refs[0][...] = peak
        out_refs[1][...] = total


def cols_kernel(packed_ref, operand_ref, peak_ref, total_ref, *out_refs):
    part = col_part_of(packed_ref[...], operand_ref)
    give_columns(merge_parts([(peak_ref[...], total_ref[...]), part]), out_refs)


def both_kernel(packed_ref, turned_ref, operand_ref, peak_ref, total_ref, rows_ref, *out_refs):
    packed = packed_ref[...]
    rows_ref[...] = row_logs_of(packed, turned_ref)
    part = col_part_of(packed, operand_ref)
    give_columns(merge_parts([(peak_ref[...], total_ref[...]), part]), out_refs)


def fold_kernel(*refs):
    count = len(refs) // 2
    arrived = refs[count][...]
    for at, (own_ref, out_ref) in enumerate(zip(refs[:count], refs[count + 1 :])):
        out_ref[...] = joined_logs([own_ref[...], arrived[at : at + 1, :]])


def joined_logs(logs):
    peak = functools.reduce(jnp.maximum, logs)
    return peak + jnp.log(sum(jnp.exp(log - peak) for log in logs))


def final_kernel(rows_count, src_base_ref, tgt_base_ref, *refs):
    logs, (src_ref, tgt_ref) = [ref[...] for ref in refs[:-2]], refs[-2:]
    src_ref[...] = 0.5 * (src_base_ref[...] - joined_logs(logs[:rows_count]))
    tgt_ref[...] = 0.5 * (tgt_base_ref[...] - joined_logs(logs[rows_count:]))


def kernel_call(body, out_shape, flops=1 << 16, **kw):
    return pl.pallas_call(
        body,
        out_shape=out_shape,
        compiler_params=pltpu.CompilerParams(vmem_limit_bytes=16 << 20),
        cost_estimate=pl.CostEstimate(
            flops=flops, bytes_accessed=1 << 18, transcendentals=1 << 18
        ),
        **kw,
    )


def exchange(value, axis, step):
    count = lax.axis_size(axis)
    return lax.ppermute(value, axis, [(i, i ^ step) for i in range(count)])


def on_device(
    src_spectra, tgt_spectra, log_src_weight, log_tgt_weight, src_potential, tgt_potential
):
  bands, rows = src_spectra.shape
  columns = tgt_spectra.shape[1]
  depth = bands + EXTRA
  f32 = functools.partial(jax.ShapeDtypeStruct, dtype=jnp.float32)
  bf16 = functools.partial(jax.ShapeDtypeStruct, dtype=jnp.bfloat16)
  flat = lambda value: value.reshape(1, -1)
  tile_flops = 4 * rows * columns * depth
  count = lax.axis_size("blk")
  order = PHASE1 if count == 4 else range(count - 1, 0, -1)

  packed, src_base = kernel_call(
      pack_kernel,
      (bf16((depth, rows)), f32((1, rows))),
      in_specs=[HBM] * 3,
      scratch_shapes=[
          pltpu.VMEM((bands, rows), jnp.bfloat16),
          pltpu.VMEM((1, rows), jnp.float32),
          pltpu.VMEM((1, rows), jnp.float32),
          pltpu.SemaphoreType.DMA((3,)),
      ],
  )(*(pltpu.with_memory_space_constraint(v, pltpu.HBM) for v in (src_spectra, flat(log_src_weight), flat(src_potential))))
  arrived = {step: exchange(packed, "blk", step) for step in order}
  turned, operand, home_rows, peak, total, tgt_base = kernel_call(
      home_kernel,
      (
          bf16((columns, depth)), bf16((depth, columns)), f32((1, rows)),
          f32((1, columns)), f32((1, columns)), f32((1, columns)),
      ),
      tile_flops,
  )(packed, tgt_spectra, flat(log_tgt_weight), flat(tgt_potential))
  held = [peak, total]
  logs = {0: home_rows}
  bits = list(BASIS) if count == 4 else [1 << at for at in range(count.bit_length() - 1)]
  lead = [step for step in order if step & bits[0]]
  rest_steps = [step for step in order if not step & bits[0]]
  col_shapes = lambda last: (f32((1, columns)),) * (1 if last else 2)

  def both(step, last):
      rows_out, *cols_out = kernel_call(
          both_kernel, (f32((1, rows)),) + col_shapes(last), tile_flops
      )(arrived[step], turned, operand, *held)
      return rows_out, cols_out

  def cols(step, last):
      return kernel_call(cols_kernel, col_shapes(last), tile_flops // 2)(
          arrived[step], operand, *held
      )

  def rows_of(step, *more):
      return kernel_call(rows_kernel, f32((1 + len(more), rows)), tile_flops // 2)(
          arrived[step], turned, *more
      )

  for step in lead[:-1]:
      logs[step], held = both(step, False)
  keys = [lead[-1]] + lead[:-1]
  parcel = rows_of(lead[-1], *(logs.pop(step) for step in lead[:-1]))
  landed = exchange(parcel, "blk", bits[0])
  held = cols(lead[-1], not rest_steps)
  for step in rest_steps[:-1]:
      logs[step], held = both(step, False)
  if rest_steps:
      held = cols(rest_steps[-1], True)
  here = held[0]
  there = exchange(here, "rep", 1)
  if rest_steps:
      logs[rest_steps[-1]] = rows_of(rest_steps[-1])
  here = joined_logs([here, there])
  col_logs = [here, exchange(here, "rep", 2)]
  for at, bit in enumerate(bits):
      own = [logs[key ^ bit] for key in keys]
      home_at = keys.index(bit)
      if len(bits) == at + 1:
          row_logs = [own[0], landed]
          break
      folded = kernel_call(fold_kernel, (f32((1, rows)),) * len(keys))(*own, landed)
      logs = {key ^ bit: value for key, value in zip(keys, folded)}
      keys = [key for key in logs if key & bits[at + 1]]
      parcel = [logs[key] for key in keys]
      parcel = parcel[0] if len(parcel) == 1 else jnp.concatenate(parcel, axis=0)
      landed = exchange(parcel, "blk", bits[at + 1])
  src_updated, tgt_updated = kernel_call(
      functools.partial(final_kernel, len(row_logs)), (f32((1, rows)), f32((1, columns)))
  )(src_base, tgt_base, *row_logs, *col_logs)
  return src_updated.reshape(-1), tgt_updated.reshape(-1)


def solution(mesh):
    placed = (
        P(None, ("pair", "rep", "blk")),
        P(None, ("pair", "blk")),
        P(("pair", "rep", "blk")),
        P(("pair", "blk")),
        P(("pair", "rep", "blk")),
        P(("pair", "blk")),
    )
    return jax.shard_map(
        on_device,
        mesh=mesh,
        in_specs=placed,
        out_specs=(P(("pair", "rep", "blk")), P(("pair", "blk"))),
        check_vma=False,
    )
```

time: 29.4 us -> 21.9 us (0.74)
  Pallas kernels: 8.34 us -> 4.7 us
  local copies, waits for them, and re-layouts: 2.04 us -> 0.01 us
  starting transfers between devices: 10.8 us -> 10 us
  other arithmetic: 0.7 us -> 0.03 us
    pallas_call x4 -> x9, Pallas kernels: 8.34 us -> 4.7 us  [the longest x2 0.94 us: cols(): kernel_call(cols_kernel, col_shapes(last), tile_flops // 2)]
    unnamed x22 -> x6, local copies, waits for them, and re-layouts: 2.04 us -> 0.01 us
    ppermute x8 -> x7, starting transfers between devices: 10.8 us -> 10 us  [exchange(): return lax.ppermute(value, axis, [(i, i ^ step) for i in range(count)])]
    add x1, other arithmetic: 0.7 us -> 0.03 us  [joined_logs(): return peak + jnp.log(sum((jnp.exp(log - peak) for log in logs)))]
    ppermute x8 -> x7, waiting for transfers between devices: 6.58 us -> 6.31 us  [exchange(): return lax.ppermute(value, axis, [(i, i ^ step) for i in range(count)])]
  transfers between devices with their start and end apart: 8 -> 7, of which waited for: 5 -> 4; matrix products, arithmetic and copies ran while one was open for 0% -> 0% of each run, Pallas kernels for 8% -> 13%
where the time goes in v2:
time: 21.9 us; the launch traced here: 21.8 us
  starting transfers between devices  10 us (46%)
  waiting for transfers between devices  6.31 us (29%)
  Pallas kernels  4.7 us (21%)
  between operations  0.69 us (3%)
    ppermute x7, starting transfers between devices, exchange(): return lax.ppermute(value, axis, [(i, i ^ step) for i in range(count)])  10 us
    ppermute x7, waiting for transfers between devices, exchange(): return lax.ppermute(value, axis, [(i, i ^ step) for i in range(count)])  6.31 us
    pallas_call x2, Pallas kernels, cols(): kernel_call(cols_kernel, col_shapes(last), tile_flops // 2)  0.94 us
    pallas_call x1, Pallas kernels, on_device(): kernel_call(pack_kernel, (bf16((depth, rows)), f32((1, rows))), in_specs=...  0.86 us
    pallas_call x2, Pallas kernels, rows_of(): kernel_call(rows_kernel, f32((1 + len(more), rows)), tile_flops // 2)  0.83 us
    pallas_call x1, Pallas kernels, on_device(): kernel_call(home_kernel, (bf16((columns, depth)), bf16((depth, columns)),...  0.78 us
    pallas_call x1, Pallas kernels, both(): kernel_call(both_kernel, (f32((1, rows)),) + col_shapes(last), tile_flops)  0.65 us
    pallas_call x1, Pallas kernels, on_device(): kernel_call(functools.partial(final_kernel, len(row_logs)), (f32((1, rows...  0.62 us
  transfers between devices with their start and end apart: 7, of which 4 were waited for; matrix products, arithmetic and copies ran while one was open for 0% of the time, Pallas kernels for 13%

profile of v2, /device:TPU:0, one launch (start us, length us, event | category | flops | bytes accessed | tf_op | source)
XLA Modules:
  0.0 21.8 jit_solution(16266337718574477810)
XLA Ops:
  0.6 0.0 copy-start
  0.7 0.9 %shard_map.77 = (bf16[72,256]{1,0:T(8,128)(2,1)S(1)}, f32[1,256]{1,0:T(1,128)S(1)}) custom-call(bf16[64,256]{1,0:T(8,128)(2,1)} %spectra_hbm.1, f32[1,256]{1,0:T(1,128)} %bitcast.8, f32[1,256]{1,0:T(1,128)} %bitcast.9), custom_call_target="tpu_custom_call" | custom-call | flops 65536 | bytes 262144 | tf_op jit(solution)/shard_map/pallas_call | solution.py:198
  1.5 0.0 copy-start.1
  1.5 5.1 %collective-permute-start.2 = (bf16[72,256]{1,0:T(8,128)(2,1)S(1)}, bf16[72,256]{1,0:T(8,128)(2,1)S(1)}, u32[]{:S(2)}, u32[]{:S(2)}) collective-permute-start(bf16[72,256]{1,0:T(8,128)(2,1)S(1)} %get-tuple-element.20.packed_ref), channel_id=1, source_target_pairs={{0,3},{1,2},{2,1},{3,0},{4,7},{5,6},{6,5},{7,4},{8,11},{9,10},{10,... | collective-permute-start | bytes 110600 | tf_op jit(solution)/shard_map/ppermute | solution.py:182
  6.7 0.0 collective-permute-start.1
  6.7 0.6 %collective-permute-start = (bf16[72,256]{1,0:T(8,128)(2,1)S(1)}, bf16[72,256]{1,0:T(8,128)(2,1)S(1)}, u32[]{:S(2)}, u32[]{:S(2)}) collective-permute-start(bf16[72,256]{1,0:T(8,128)(2,1)S(1)} %get-tuple-element.20.packed_ref), channel_id=1, source_target_pairs={{0,2},{1,3},{2,0},{3,1},{4,6},{5,7},{6,4},{7,5},{8,10},{9,11},{10,... | collective-permute-start | bytes 110600 | tf_op jit(solution)/shard_map/ppermute | solution.py:182
  7.3 0.8 %shard_map.78 = (bf16[1024,72]{1,0:T(8,128)(2,1)S(1)}, bf16[72,1024]{1,0:T(8,128)(2,1)S(1)}, f32[1,256]{1,0:T(1,128)S(1)}, f32[1,1024]{1,0:T(1,128)S(1)}, f32[1,1024]{1,0:T(1,128)S(1)}, /*index=5*/f32[1,1024]{1,0:T(1,128)S(1)}) custom-call(bf16[72,256]{1,0:T(8,128)(2,1)S(1)} %get-tuple-element.20.packed_ref, bf16[64,1024]{1,0:T(8,128)(2,1)S(1)} %copy-done, ...), custom_call_target="tpu_custom_call" | custom-call | flops 75497472 | bytes 262144 | tf_op jit(solution)/shard_map/pallas_call | solution.py:210
  8.1 0.5 %collective-permute-done.2.packed_ref = bf16[72,256]{1,0:T(8,128)(2,1)S(1)} collective-permute-done((bf16[72,256]{1,0:T(8,128)(2,1)S(1)}, bf16[72,256]{1,0:T(8,128)(2,1)S(1)}, u32[]{:S(2)}, u32[]{:S(2)}) %collective-permute-start.2) | collective-permute-done | bytes 36896 | tf_op jit(solution)/shard_map/ppermute | solution.py:182
  8.6 0.7 %shard_map.80 = (f32[1,256]{1,0:T(1,128)S(1)}, f32[1,1024]{1,0:T(1,128)S(1)}, f32[1,1024]{1,0:T(1,128)S(1)}) custom-call(bf16[72,256]{1,0:T(8,128)(2,1)S(1)} %collective-permute-done.2.packed_ref, bf16[1024,72]{1,0:T(8,128)(2,1)S(1)} %get-tuple-element.23.turned_ref, bf16[72,1024]{1,0:T(8,128)(2,1)S(1)} %get-tuple-element.24.operand_ref, ...), custom_call_target="tpu_custom_call" | custom-call | flops 75497472 | bytes 262144 | tf_op jit(solution)/shard_map/pallas_call | solution.py:226
  9.3 1.4 %collective-permute-done.1.packed_ref = bf16[72,256]{1,0:T(8,128)(2,1)S(1)} collective-permute-done((bf16[72,256]{1,0:T(8,128)(2,1)S(1)}, bf16[72,256]{1,0:T(8,128)(2,1)S(1)}, u32[]{:S(2)}, u32[]{:S(2)}) %collective-permute-start.1) | collective-permute-done | bytes 36896 | tf_op jit(solution)/shard_map/ppermute | solution.py:182
  10.6 0.5 %shard_map.83 = (f32[1,1024]{1,0:T(1,128)S(1)}, f32[1,1024]{1,0:T(1,128)S(1)}) custom-call(bf16[72,256]{1,0:T(8,128)(2,1)S(1)} %collective-permute-done.1.packed_ref, bf16[72,1024]{1,0:T(8,128)(2,1)S(1)} %get-tuple-element.24.operand_ref, f32[1,1024]{1,0:T(1,128)S(1)} %get-tuple-element.30.peak_ref, f32[1,1024]{1,0:T(1,128)S(1)} %get-tuple-element.31.total_ref), custom_call_target="tpu_custom_call" | custom-call | flops 37748736 | bytes 262144 | tf_op jit(solution)/shard_map/pallas_call | solution.py:232
  11.1 0.6 %collective-permute-done.packed_ref = bf16[72,256]{1,0:T(8,128)(2,1)S(1)} collective-permute-done((bf16[72,256]{1,0:T(8,128)(2,1)S(1)}, bf16[72,256]{1,0:T(8,128)(2,1)S(1)}, u32[]{:S(2)}, u32[]{:S(2)}) %collective-permute-start) | collective-permute-done | bytes 36896 | tf_op jit(solution)/shard_map/ppermute | solution.py:182
  11.7 0.5 %shard_map.84 = f32[1,1024]{1,0:T(1,128)S(1)} custom-call(bf16[72,256]{1,0:T(8,128)(2,1)S(1)} %collective-permute-done.packed_ref, bf16[72,1024]{1,0:T(8,128)(2,1)S(1)} %get-tuple-element.24.operand_ref, f32[1,1024]{1,0:T(1,128)S(1)} %get-tuple-element.32.peak_ref, f32[1,1024]{1,0:T(1,128)S(1)} %get-tuple-element.33.total_ref), custom_call_target="tpu_custom_call" | custom-call | flops 37748736 | bytes 262144 | tf_op jit(solution)/shard_map/pallas_call | solution.py:232
  12.2 0.1 collective-permute-start.5
  12.2 0.4 %shard_map.81 = f32[2,256]{1,0:T(2,128)S(1)} custom-call(bf16[72,256]{1,0:T(8,128)(2,1)S(1)} %collective-permute-done.1.packed_ref, bf16[1024,72]{1,0:T(8,128)(2,1)S(1)} %get-tuple-element.23.turned_ref, f32[1,256]{1,0:T(1,128)S(1)} %get-tuple-element.27.refs_0_), custom_call_target="tpu_custom_call" | custom-call | flops 37748736 | bytes 262144 | tf_op jit(solution)/shard_map/pallas_call | solution.py:237
  12.7 1.9 %collective-permute-start.3 = (f32[2,256]{1,0:T(2,128)S(1)}, f32[2,256]{1,0:T(2,128)S(1)}, u32[]{:S(2)}, u32[]{:S(2)}) collective-permute-start(f32[2,256]{1,0:T(2,128)S(1)} %shard_map.81), channel_id=1, source_target_pairs={{0,1},{1,0},{2,3},{3,2},{4,5},{5,4},{6,7},{7,6},{8,9},{9,8},{10,11... | collective-permute-start | bytes 6152 | tf_op jit(solution)/shard_map/ppermute | solution.py:182
  14.6 0.0 collective-permute-done.5
  14.6 1.5 %collective-permute-start.6 = (f32[1,1024]{1,0:T(1,128)S(1)}, f32[1,1024]{1,0:T(1,128)S(1)}, u32[]{:S(2)}, u32[]{:S(2)}) collective-permute-start(f32[1,1024]{1,0:T(1,128)S(1)} %log_add_fusion.refs_2_), channel_id=1, source_target_pairs={{0,8},{4,12},{8,0},{12,4},{1,9},{5,13},{9,1},{13,5},{2,10},{6,14},... | collective-permute-start | bytes 12296 | tf_op jit(solution)/shard_map/ppermute | solution.py:182
  16.2 0.4 %shard_map.79.refs_1_ = f32[1,256]{1,0:T(1,128)S(1)} custom-call(bf16[72,256]{1,0:T(8,128)(2,1)S(1)} %collective-permute-done.packed_ref, bf16[1024,72]{1,0:T(8,128)(2,1)S(1)} %get-tuple-element.23.turned_ref), custom_call_target="tpu_custom_call" | custom-call | flops 37748736 | bytes 262144 | tf_op jit(solution)/shard_map/pallas_call | solution.py:237
  16.6 0.0 collective-permute-done.3.refs_2_
  16.6 0.7 %collective-permute-start.4 = (f32[1,256]{1,0:T(1,128)S(1)}, f32[1,256]{1,0:T(1,128)S(1)}, u32[]{:S(2)}, u32[]{:S(2)}) collective-permute-start(f32[1,256]{1,0:T(1,128)S(1)} %get-tuple-element.29), channel_id=1, source_target_pairs={{0,2},{1,3},{2,0},{3,1},{4,6},{5,7},{6,4},{7,5},{8,10},{9,11},{10,... | collective-permute-start | bytes 3080 | tf_op jit(solution)/shard_map/ppermute | solution.py:182
  17.3 3.8 %collective-permute-done.4.refs_1_ = f32[1,256]{1,0:T(1,128)S(1)} collective-permute-done((f32[1,256]{1,0:T(1,128)S(1)}, f32[1,256]{1,0:T(1,128)S(1)}, u32[]{:S(2)}, u32[]{:S(2)}) %collective-permute-start.4) | collective-permute-done | bytes 1056 | tf_op jit(solution)/shard_map/ppermute | solution.py:182
  21.2 0.0 collective-permute-done.6.refs_3_
  21.2 0.6 %shard_map.85 = (f32[1,256]{1,0:T(1,128)}, f32[1,1024]{1,0:T(1,128)}) custom-call(f32[1,256]{1,0:T(1,128)S(1)} %get-tuple-element.19.src_base_ref, f32[1,1024]{1,0:T(1,128)S(1)} %get-tuple-element.21.tgt_base_ref, f32[1,256]{1,0:T(1,128)S(1)} %get-tuple-element.28.refs_0_, f32[1,256]{1,0:T(1,128)S(1)} %collective-permute-done.4.refs_1_, ...), custom_call_target="tpu_custom_call" | custom-call | flops 65536 | bytes 262144 | tf_op jit(solution)/shard_map/pallas_call | solution.py:269
  (6 shorter events, 0.1 us)
Async XLA Ops:
  0.6 6.7 %copy-start = (bf16[64,1024]{1,0:T(8,128)(2,1)S(1)}, bf16[64,1024]{1,0:T(8,128)(2,1)}, u32[]{:S(2)}) copy-start(bf16[64,1024]{1,0:T(8,128)(2,1)} %spectra_ref.1) | copy-start | bytes 393220
  0.6 6.7 %copy-start.2 = (f32[1024]{0:T(1024)S(1)}, f32[1024]{0:T(1024)}, u32[]{:S(2)}) copy-start(f32[1024]{0:T(1024)} %param.11) | copy-start | bytes 12292
  1.5 5.8 %copy-start.1 = (f32[1024]{0:T(1024)S(1)}, f32[1024]{0:T(1024)}, u32[]{:S(2)}) copy-start(f32[1024]{0:T(1024)} %param.9) | copy-start | bytes 12292
  1.5 7.1 %collective-permute-start.2 = (bf16[72,256]{1,0:T(8,128)(2,1)S(1)}, bf16[72,256]{1,0:T(8,128)(2,1)S(1)}, u32[]{:S(2)}, u32[]{:S(2)}) collective-permute-start(bf16[72,256]{1,0:T(8,128)(2,1)S(1)} %get-tuple-element.20.packed_ref), channel_id=1, source_target_pairs={{0,3},{1,2},{2,1},{3,0},{4,7},{5,6},{6,5},{7,4},{8,11},{9,10},{10,... | collective-permute-start | bytes 110600 | tf_op jit(solution)/shard_map/ppermute | solution.py:182
  6.7 4.0 %collective-permute-start.1 = (bf16[72,256]{1,0:T(8,128)(2,1)S(1)}, bf16[72,256]{1,0:T(8,128)(2,1)S(1)}, u32[]{:S(2)}, u32[]{:S(2)}) collective-permute-start(bf16[72,256]{1,0:T(8,128)(2,1)S(1)} %get-tuple-element.20.packed_ref), channel_id=1, source_target_pairs={{0,1},{1,0},{2,3},{3,2},{4,5},{5,4},{6,7},{7,6},{8,9},{9,8},{10,11... | collective-permute-start | bytes 110600 | tf_op jit(solution)/shard_map/ppermute | solution.py:182
  6.7 5.0 %collective-permute-start = (bf16[72,256]{1,0:T(8,128)(2,1)S(1)}, bf16[72,256]{1,0:T(8,128)(2,1)S(1)}, u32[]{:S(2)}, u32[]{:S(2)}) collective-permute-start(bf16[72,256]{1,0:T(8,128)(2,1)S(1)} %get-tuple-element.20.packed_ref), channel_id=1, source_target_pairs={{0,2},{1,3},{2,0},{3,1},{4,6},{5,7},{6,4},{7,5},{8,10},{9,11},{10,... | collective-permute-start | bytes 110600 | tf_op jit(solution)/shard_map/ppermute | solution.py:182
  12.2 2.4 %collective-permute-start.5 = (f32[1,1024]{1,0:T(1,128)S(1)}, f32[1,1024]{1,0:T(1,128)S(1)}, u32[]{:S(2)}, u32[]{:S(2)}) collective-permute-start(f32[1,1024]{1,0:T(1,128)S(1)} %shard_map.84), channel_id=1, source_target_pairs={{0,4},{4,0},{8,12},{12,8},{1,5},{5,1},{9,13},{13,9},{2,6},{6,2},{1... | collective-permute-start | bytes 12296 | tf_op jit(solution)/shard_map/ppermute | solution.py:182
  12.7 3.9 %collective-permute-start.3 = (f32[2,256]{1,0:T(2,128)S(1)}, f32[2,256]{1,0:T(2,128)S(1)}, u32[]{:S(2)}, u32[]{:S(2)}) collective-permute-start(f32[2,256]{1,0:T(2,128)S(1)} %shard_map.81), channel_id=1, source_target_pairs={{0,1},{1,0},{2,3},{3,2},{4,5},{5,4},{6,7},{7,6},{8,9},{9,8},{10,11... | collective-permute-start | bytes 6152 | tf_op jit(solution)/shard_map/ppermute | solution.py:182
  14.6 6.5 %collective-permute-start.6 = (f32[1,1024]{1,0:T(1,128)S(1)}, f32[1,1024]{1,0:T(1,128)S(1)}, u32[]{:S(2)}, u32[]{:S(2)}) collective-permute-start(f32[1,1024]{1,0:T(1,128)S(1)} %log_add_fusion.refs_2_), channel_id=1, source_target_pairs={{0,8},{4,12},{8,0},{12,4},{1,9},{5,13},{9,1},{13,5},{2,10},{6,14},... | collective-permute-start | bytes 12296 | tf_op jit(solution)/shard_map/ppermute | solution.py:182
  16.6 4.5 %collective-permute-start.4 = (f32[1,256]{1,0:T(1,128)S(1)}, f32[1,256]{1,0:T(1,128)S(1)}, u32[]{:S(2)}, u32[]{:S(2)}) collective-permute-start(f32[1,256]{1,0:T(1,128)S(1)} %get-tuple-element.29), channel_id=1, source_target_pairs={{0,2},{1,3},{2,0},{3,1},{4,6},{5,7},{6,4},{7,5},{8,10},{9,11},{10,... | collective-permute-start | bytes 3080 | tf_op jit(solution)/shard_map/ppermute | solution.py:182
